TPU v7x, 8 devices: a whole 2x2x1 slice. The times are simulated.
8 devices in a mesh: seqs: 2 (over z, y), states: 4 (over x, core).
Axes of the slice: x: 2, y: 2, z: 1, core: 2. Of those that a mesh axis runs over, the one named last changes fastest.
Arguments:
- trans_mat: bfloat16 [8192, 8192], P(None, 'states')
- emit_mat: bfloat16 [8192, 10000], P('states')
- init_prob: float32 [8192], P('states')
- tokens: int32 [64, 64], P('seqs'), parts along dimension 0
- lengths: int32 [64], P('seqs'), parts along dimension 0
Outputs:
- output 1: float32 [64], P('seqs'), parts along dimension 0
- output 2: float32 [64, 8192], P('seqs', 'states'), parts along dimension 0
- output 3: float32 [16384, 2048], P(('seqs', 'states')), parts along dimension 0
There are 2 independent parts. A program takes and returns all parts, laid end to end along the dimension named above; an argument that names none is the same for every part.
All inputs are finite; a program needn't handle non-finite values.
Results may differ from a plain program's by a relative error of at most 0.001.
Values are sent between devices in bfloat16 or wider.
A program may use at most 1 GiB of HBM per device.

v0:
```python
import jax
import jax.numpy as jnp
from jax import lax
from jax.sharding import PartitionSpec as P


def solution(mesh):
    def step_weight(live_mask, emit_now, beta_cur, step_scale):
        scaled = emit_now.astype(jnp.float32) * beta_cur / step_scale[:, None]
        return jnp.where(live_mask[:, None], scaled, 0.0).astype(jnp.bfloat16)

    def local_run(trans_loc, emit_loc, init_loc, tokens_loc, lengths_loc):
        seq_count, step_count = tokens_loc.shape
        block_size = trans_loc.shape[1]
        group_idx = lax.axis_index('states')
        emit_seq = jnp.transpose(jnp.take(emit_loc, tokens_loc.T, axis=1), (1, 2, 0))
        first_mass = init_loc[None, :] * emit_seq[0].astype(jnp.float32)
        first_norm = lax.psum(jnp.sum(first_mass, axis=1), 'states')
        alpha_first = first_mass / first_norm[:, None]
        live_steps = jnp.arange(1, step_count)[:, None] < lengths_loc[None, :]

        def forward_step(alpha_cur, inputs):
            live_mask, emit_now = inputs
            alpha_bf = alpha_cur.astype(jnp.bfloat16)
            alpha_full = lax.all_gather(alpha_bf, 'states', axis=1, tiled=True)
            pred_mass = jnp.dot(alpha_full, trans_loc, preferred_element_type=jnp.float32)
            new_mass = pred_mass * emit_now.astype(jnp.float32)
            norm_sum = lax.psum(jnp.sum(new_mass, axis=1), 'states')
            step_scale = jnp.where(live_mask, norm_sum, 1.0)
            alpha_next = jnp.where(live_mask[:, None], new_mass / norm_sum[:, None], alpha_cur)
            return alpha_next, (alpha_bf, step_scale)

        alpha_last, (alpha_prev, scales) = lax.scan(forward_step, alpha_first, (live_steps, emit_seq[1:]))
        loglik = jnp.log(first_norm) + jnp.sum(jnp.log(scales), axis=0)

        def backward_step(beta_cur, inputs):
            live_mask, emit_now, step_scale = inputs
            weight = step_weight(live_mask, emit_now, beta_cur, step_scale)
            partial_sum = lax.dot_general(weight, trans_loc, (((1,), (1,)), ((), ())), preferred_element_type=jnp.float32)
            beta_prev = lax.psum_scatter(partial_sum, 'states', scatter_dimension=1, tiled=True)
            return beta_prev + jnp.where(live_mask, 0.0, 1.0)[:, None], weight

        beta_one, late_weights = lax.scan(backward_step, jnp.ones((seq_count, block_size), jnp.float32), (live_steps[1:], emit_seq[2:], scales[1:]), reverse=True)
        first_weight = step_weight(live_steps[0], emit_seq[1], beta_one, scales[0])
        pair_sum = jnp.einsum('tbi,tbj->ij', alpha_prev[1:], late_weights, preferred_element_type=jnp.float32)
        pair_sum = pair_sum + lax.dot_general(alpha_prev[0], first_weight, (((0,), (0,)), ((), ())), preferred_element_type=jnp.float32)
        diag_block = lax.dynamic_slice_in_dim(trans_loc, group_idx * block_size, block_size, axis=0)
        counts = diag_block.astype(jnp.float32) * pair_sum
        return loglik, alpha_last, counts

    return jax.shard_map(local_run, mesh=mesh, in_specs=(P(None, 'states'), P('states', None), P('states'), P('seqs', None), P('seqs')), out_specs=(P('seqs'), P('seqs', 'states'), P(('seqs', 'states'), None)), check_vma=False)
```

profile of v0, /device:TPU:0, one launch (start us, length us, event | category | flops | bytes accessed | tf_op | source)
XLA Modules:
  0.0 4417.0 jit_solution(9846181323573129292)
XLA Ops:
  10.8 47.9 %gather_fusion = bf16[2048,2048]{1,0:T(8,128)(2,1)} fusion(bf16[2048,10000]{0,1:T(8,128)(2,1)} %param.10, s32[2048]{0:T(1024)S(1)} %broadcast_clamp_fusion), kind=kCustom, calls=%fused_computation | custom fusion | bytes 16785408 | tf_op jit(solution)/shard_map/jit(_take)/gather | solution.py:16
  93.4 1917.2 %while.31 = (s32[]{:T(128)}, f32[32,2048]{1,0:T(8,128)S(1)}, bf16[63,32,2048]{2,1,0:T(8,128)(2,1)}, f32[63,32]{1,0:T(8,128)S(1)}, pred[63,32]{1,0:T(8,128)(4,1)}...) while((s32[]{:T(128)}, f32[32,2048]{1,0:T(8,128)S(1)}, ...), condition=%wide.region_5.6_spmd, body=%wide.region_2.0_spmd.sunk | while | flops 1074135040 | bytes 36439252 | solution.py:33
  2015.5 2316.4 %while.32 = (s32[]{:T(128)}, f32[32,2048]{1,0:T(8,128)S(1)}, bf16[62,32,2048]{2,1,0:T(8,128)(2,1)}, pred[62,32]{1,0:T(8,128)(4,1)}, bf16[62,32,2048]{2,1,0:T(8,1...) while((s32[]{:T(128)}, f32[32,2048]{1,0:T(8,128)S(1)}, ...), condition=%wide.region_9.10_spmd.clone, body=%wide.region_7.9_spmd.clone.sunk | while | flops 1074593792 | bytes 39978032 | solution.py:43
  2034.1 18.7 reduce-scatter.2.cloned.1.call-done
  2072.5 17.6 reduce-scatter.2.cloned.1.call-done
  2109.8 17.6 reduce-scatter.2.cloned.1.call-done
  2147.1 17.6 reduce-scatter.2.cloned.1.call-done
  2221.7 17.7 reduce-scatter.2.cloned.1.call-done
  2259.0 17.6 reduce-scatter.2.cloned.1.call-done
  2296.3 17.6 reduce-scatter.2.cloned.1.call-done
  2333.6 17.6 reduce-scatter.2.cloned.1.call-done
  2408.3 17.6 reduce-scatter.2.cloned.1.call-done
  2482.8 17.6 reduce-scatter.2.cloned.1.call-done
  2520.2 17.6 reduce-scatter.2.cloned.1.call-done
  2557.5 17.6 reduce-scatter.2.cloned.1.call-done
  2594.9 17.6 reduce-scatter.2.cloned.1.call-done
  2669.6 17.6 reduce-scatter.2.cloned.1.call-done
  2707.0 17.6 reduce-scatter.2.cloned.1.call-done
  2744.4 17.6 reduce-scatter.2.cloned.1.call-done
  2781.7 17.6 reduce-scatter.2.cloned.1.call-done
  2819.1 17.6 reduce-scatter.2.cloned.1.call-done
  2893.8 17.6 reduce-scatter.2.cloned.1.call-done
  3006.0 17.6 reduce-scatter.2.cloned.1.call-done
  3043.4 17.6 reduce-scatter.2.cloned.1.call-done
  3155.5 17.6 reduce-scatter.2.cloned.1.call-done
  3192.8 17.6 reduce-scatter.2.cloned.1.call-done
  3230.1 17.6 reduce-scatter.2.cloned.1.call-done
  3267.4 17.6 reduce-scatter.2.cloned.1.call-done
  3304.8 17.6 reduce-scatter.2.cloned.1.call-done
  3342.1 17.6 reduce-scatter.2.cloned.1.call-done
  3379.4 17.6 reduce-scatter.2.cloned.1.call-done
  3416.7 17.6 reduce-scatter.2.cloned.1.call-done
  3454.0 17.6 reduce-scatter.2.cloned.1.call-done
  3491.3 17.6 reduce-scatter.2.cloned.1.call-done
  3565.9 17.6 reduce-scatter.2.cloned.1.call-done
  3603.3 17.6 reduce-scatter.2.cloned.1.call-done
  3640.6 17.6 reduce-scatter.2.cloned.1.call-done
  3677.9 17.6 reduce-scatter.2.cloned.1.call-done
  3752.5 17.6 reduce-scatter.2.cloned.1.call-done
  3827.3 17.6 reduce-scatter.2.cloned.1.call-done
  3902.0 17.6 reduce-scatter.2.cloned.1.call-done
  3939.4 17.6 reduce-scatter.2.cloned.1.call-done
  4014.2 17.6 reduce-scatter.2.cloned.1.call-done
  4088.9 17.6 reduce-scatter.2.cloned.1.call-done
  4163.6 17.6 reduce-scatter.2.cloned.1.call-done
  4201.0 17.6 reduce-scatter.2.cloned.1.call-done
  4238.3 17.6 reduce-scatter.2.cloned.1.call-done
  4343.1 50.5 %fusion.7 = f32[2048,2048,1]{1,0,2:T(8,128)} fusion(bf16[63,32,2048]{2,0,1:T(8,128)(2,1)} %copy.13, bf16[62,32,2048]{2,1,0:T(8,128)(2,1)} %get-tuple-element.187), kind=kOutput, calls=%fused_computation.19 | convolution fusion | flops 16642998272 | bytes 33161216 | tf_op jit(solution)/shard_map/tbi,tbj->ij/dot_general | solution.py:45
  (929 shorter events, 3523.1 us)
Async XLA Ops:
  2015.5 37.3 reduce-scatter.2.cloned.1.call-start
  2053.8 36.3 reduce-scatter.2.cloned.1.call-start
  2091.1 36.3 reduce-scatter.2.cloned.1.call-start
  2128.5 36.3 reduce-scatter.2.cloned.1.call-start
  2203.1 36.3 reduce-scatter.2.cloned.1.call-start
  2277.7 36.3 reduce-scatter.2.cloned.1.call-start
  2315.0 36.3 reduce-scatter.2.cloned.1.call-start
  2352.3 36.3 reduce-scatter.2.cloned.1.call-start
  2538.9 36.3 reduce-scatter.2.cloned.1.call-start
  2576.2 36.3 reduce-scatter.2.cloned.1.call-start
  2613.6 36.3 reduce-scatter.2.cloned.1.call-start
  2650.9 36.3 reduce-scatter.2.cloned.1.call-start
  2688.3 36.3 reduce-scatter.2.cloned.1.call-start
  2725.7 36.3 reduce-scatter.2.cloned.1.call-start
  2763.0 36.3 reduce-scatter.2.cloned.1.call-start
  2800.4 36.3 reduce-scatter.2.cloned.1.call-start
  2837.8 36.3 reduce-scatter.2.cloned.1.call-start
  2875.1 36.3 reduce-scatter.2.cloned.1.call-start
  2912.5 36.3 reduce-scatter.2.cloned.1.call-start
  2949.9 36.3 reduce-scatter.2.cloned.1.call-start
  2987.3 36.3 reduce-scatter.2.cloned.1.call-start
  3024.7 36.3 reduce-scatter.2.cloned.1.call-start
  3062.1 36.3 reduce-scatter.2.cloned.1.call-start
  3099.5 36.3 reduce-scatter.2.cloned.1.call-start
  3136.8 36.3 reduce-scatter.2.cloned.1.call-start
  3174.2 36.3 reduce-scatter.2.cloned.1.call-start
  3211.5 36.3 reduce-scatter.2.cloned.1.call-start
  3248.8 36.3 reduce-scatter.2.cloned.1.call-start
  3286.1 36.3 reduce-scatter.2.cloned.1.call-start
  3323.4 36.3 reduce-scatter.2.cloned.1.call-start
  3360.8 36.3 reduce-scatter.2.cloned.1.call-start
  3398.1 36.3 reduce-scatter.2.cloned.1.call-start
  3733.9 36.3 reduce-scatter.2.cloned.1.call-start
  3771.2 36.3 reduce-scatter.2.cloned.1.call-start
  3808.6 36.3 reduce-scatter.2.cloned.1.call-start
  3846.0 36.3 reduce-scatter.2.cloned.1.call-start
  3883.3 36.3 reduce-scatter.2.cloned.1.call-start
  3920.7 36.3 reduce-scatter.2.cloned.1.call-start
  3958.1 36.3 reduce-scatter.2.cloned.1.call-start
  3995.5 36.3 reduce-scatter.2.cloned.1.call-start
  4032.9 36.3 reduce-scatter.2.cloned.1.call-start
  4070.2 36.3 reduce-scatter.2.cloned.1.call-start
  4107.6 36.3 reduce-scatter.2.cloned.1.call-start
  4145.0 36.3 reduce-scatter.2.cloned.1.call-start
  4182.3 36.3 reduce-scatter.2.cloned.1.call-start
  4219.7 36.3 reduce-scatter.2.cloned.1.call-start
  4257.0 36.3 reduce-scatter.2.cloned.1.call-start
  4294.4 36.3 reduce-scatter.2.cloned.1.call-start
  (19 other events, 2493.6 us)
Sparse Core Ops, SparseCore 0:
  2032.5 20.1 reduce-scatter.1
  2108.2 19.1 reduce-scatter.1
  2145.6 19.1 reduce-scatter.1
  2220.2 19.1 reduce-scatter.1
  2257.5 19.1 reduce-scatter.1
  2294.8 19.1 reduce-scatter.1
  2332.1 19.1 reduce-scatter.1
  2369.4 19.1 reduce-scatter.1
  2406.7 19.1 reduce-scatter.1
  2444.0 19.1 reduce-scatter.1
  2481.3 19.1 reduce-scatter.1
  2518.6 19.1 reduce-scatter.1
  2556.0 19.1 reduce-scatter.1
  2593.4 19.1 reduce-scatter.1
  2630.7 19.1 reduce-scatter.1
  2668.1 19.1 reduce-scatter.1
  2705.4 19.1 reduce-scatter.1
  2742.8 19.1 reduce-scatter.1
  2780.2 19.1 reduce-scatter.1
  2817.5 19.1 reduce-scatter.1
  2854.9 19.1 reduce-scatter.1
  2892.3 19.1 reduce-scatter.1
  2929.7 19.1 reduce-scatter.1
  2967.1 19.1 reduce-scatter.1
  3004.5 19.1 reduce-scatter.1
  3041.8 19.1 reduce-scatter.1
  3079.2 19.1 reduce-scatter.1
  3116.6 19.1 reduce-scatter.1
  3153.9 19.1 reduce-scatter.1
  3191.3 19.1 reduce-scatter.1
  3228.6 19.1 reduce-scatter.1
  3265.9 19.1 reduce-scatter.1
  3303.2 19.1 reduce-scatter.1
  3340.5 19.1 reduce-scatter.1
  3377.9 19.1 reduce-scatter.1
  3415.2 19.1 reduce-scatter.1
  3452.5 19.1 reduce-scatter.1
  3489.8 19.1 reduce-scatter.1
  3527.1 19.1 reduce-scatter.1
  3564.4 19.1 reduce-scatter.1
  3601.7 19.1 reduce-scatter.1
  3639.0 19.1 reduce-scatter.1
  3676.3 19.1 reduce-scatter.1
  3713.6 19.1 reduce-scatter.1
  3863.1 19.1 reduce-scatter.1
  4012.6 19.1 reduce-scatter.1
  4050.0 19.1 reduce-scatter.1
  4087.4 19.1 reduce-scatter.1
  (14 shorter events, 267.0 us)
where the time goes:
time: 4430 us; the launch traced here: 4420 us
  matrix products  1940 us (44%)
  waiting for transfers between devices  1100 us (25%)
  blocking collectives  965 us (22%)
  other arithmetic  312 us (7%)
  local copies, waits for them, and re-layouts  84.1 us (2%)
    reduce_scatter x62, waiting for transfers between devices, backward_step(): lax.psum_scatter(partial_sum, 'states', scatter_dimension=1, tiled=True)  1090 us
    dot_general x62, matrix products, backward_step(): lax.dot_general(weight, trans_loc, (((1,), (1,)), ((), ())), preferred_el...  1010 us
    dot_general x63, matrix products, forward_step(): jnp.dot(alpha_full, trans_loc, preferred_element_type=jnp.float32)  864 us
    all_gather x63, blocking collectives, forward_step(): alpha_full = lax.all_gather(alpha_bf, 'states', axis=1, tiled=True)  600 us
    psum x63, blocking collectives, forward_step(): norm_sum = lax.psum(jnp.sum(new_mass, axis=1), 'states')  357 us
    dynamic_update_slice x62, other arithmetic, local_run(): lax.scan(backward_step, jnp.ones((seq_count, block_size), jnp.float32), (...  103 us
  transfers between devices with their start and end apart: 62, of which 62 were waited for; matrix products, arithmetic and copies ran while one was open for 2% of the time, Pallas kernels for 0%

commit v1 on v0

--- a/solution.py
+++ b/solution.py
@@ -1,7 +1,180 @@
+import functools
+
 import jax
 import jax.numpy as jnp
 from jax import lax
+from jax.experimental import pallas as pl
+from jax.experimental.pallas import tpu as pltpu
 from jax.sharding import PartitionSpec as P
+
+MESH = pl.DeviceIdType.MESH
+CHUNKS = 4
+LOADS = 8
+
+
+def peers(me):
+    return me + 1 - 2 * (me % 2), 3 - me, 3 - (me + 1 - 2 * (me % 2))
+
+
+def entry_barrier(others):
+    barrier = pltpu.get_barrier_semaphore()
+    for other in others:
+        pl.semaphore_signal(barrier, inc=1, device_id=other, device_id_type=MESH)
+    pl.semaphore_wait(barrier, len(others))
+
+
+def exchange_matmul(me, slot, xbuf, mat, acc, send_sem, recv_sem):
+    partner, cross, far = peers(me)
+    block = xbuf.shape[3]
+    width = block // CHUNKS
+
+    def part(owner, c):
+        return xbuf.at[slot, owner, :, pl.ds(c * width, width)]
+
+    def copy(owner, c, kind, device):
+        ref = part(owner, c)
+        return pltpu.make_async_remote_copy(
+            src_ref=ref, dst_ref=ref, send_sem=send_sem.at[slot, kind, c], recv_sem=recv_sem.at[slot, kind, c],
+            device_id={"states": device}, device_id_type=MESH)
+
+    sends = []
+    for c in range(CHUNKS):
+        out = copy(me, c, 1, cross)
+        out.start()
+        sends.append(out)
+        out = copy(me, c, 0, partner)
+        out.start()
+        sends.append(out)
+
+    def dot(owner, lo, size):
+        rows = pl.ds(pl.multiple_of(owner * block + lo, width), size)
+        return jnp.dot(xbuf[slot, owner, :, pl.ds(lo, size)], mat[rows, :], preferred_element_type=jnp.float32)
+
+    acc[...] = dot(me, 0, block)
+    for c in range(CHUNKS):
+        copy(partner, c, 0, partner).wait_recv()
+    acc[...] += dot(partner, 0, block)
+
+    def relay(c):
+        copy(cross, c, 1, cross).wait_recv()
+        out = copy(cross, c, 2, partner)
+        out.start()
+        sends.append(out)
+
+    for c in range(CHUNKS):
+        relay(c)
+        acc[...] += dot(cross, c * width, width)
+        if c:
+            copy(far, c - 1, 2, partner).wait_recv()
+            acc[...] += dot(far, (c - 1) * width, width)
+    copy(far, CHUNKS - 1, 2, partner).wait_recv()
+    acc[...] += dot(far, (CHUNKS - 1) * width, width)
+    return sends
+
+
+def packed(col):
+    group = lax.broadcasted_iota(jnp.int32, (8, 128), 1) // 32
+    out = jnp.broadcast_to(col[24:32], (8, 128))
+    for k in range(3):
+        out = jnp.where(group == k, jnp.broadcast_to(col[8 * k:8 * k + 8], (8, 128)), out)
+    return out
+
+
+def unpacked(tile):
+    return jnp.concatenate([tile[:, 32 * k:32 * k + 1] for k in range(4)], axis=0)
+
+
+def forward_kernel(emit_ref, init_ref, len_col, len_pack, a_hbm, hist_ref, scale_ref, log_ref, post_ref,
+                   mat, xbuf, acc, cbuf, load_sem, send_sem, recv_sem, csend_sem, crecv_sem):
+    me = lax.axis_index("states")
+    partner, cross, far = peers(me)
+    rows = mat.shape[0] // LOADS
+    loads = [pltpu.make_async_copy(a_hbm.at[pl.ds(k * rows, rows)], mat.at[pl.ds(k * rows, rows)], load_sem.at[k]) for k in range(LOADS)]
+    for load in loads:
+        load.start()
+    entry_barrier([{"states": partner}, {"states": cross}, {"states": far}])
+
+    def norm_total(mass):
+        cbuf[me] = packed(jnp.sum(mass, axis=1, keepdims=True))
+
+        def copy(owner, kind, device):
+            return pltpu.make_async_remote_copy(
+                src_ref=cbuf.at[owner], dst_ref=cbuf.at[owner], send_sem=csend_sem.at[kind], recv_sem=crecv_sem.at[kind],
+                device_id={"states": device}, device_id_type=MESH)
+
+        others = (far, cross, partner)
+        for kind, other in enumerate(others):
+            copy(me, kind, other).start()
+        for kind, other in enumerate(others):
+            copy(other, kind, other).wait_recv()
+        for kind, other in enumerate(others):
+            copy(me, kind, other).wait_send()
+        return cbuf[0] + cbuf[1] + cbuf[2] + cbuf[3]
+
+    mass = init_ref[...] * emit_ref[0].astype(jnp.float32)
+    total = norm_total(mass)
+    scale_ref[0] = total
+    log_ref[...] = jnp.log(total)
+    alpha = mass * unpacked(1.0 / total)
+    post_ref[...] = alpha
+    xbuf[0, me] = alpha.astype(jnp.bfloat16)
+    hist_ref[0] = alpha.astype(jnp.bfloat16)
+    for load in loads:
+        load.wait()
+
+    def step(t, carry):
+        slot = (t - 1) % 2
+        sends = exchange_matmul(me, slot, xbuf, mat, acc, send_sem, recv_sem)
+        mass = acc[...] * emit_ref[t].astype(jnp.float32)
+        acc[...] = mass
+        total = norm_total(mass)
+        live = t < len_pack[...]
+        scale = jnp.where(live, total, 1.0)
+        scale_ref[t] = scale
+        log_ref[...] += jnp.log(scale)
+        alpha = jnp.where(t < len_col[...], acc[...] * unpacked(1.0 / total), post_ref[...])
+        post_ref[...] = alpha
+        xbuf[t % 2, me] = alpha.astype(jnp.bfloat16)
+        hist_ref[t] = alpha.astype(jnp.bfloat16)
+        for send in sends:
+            send.wait_send()
+        return carry
+
+    lax.fori_loop(1, emit_ref.shape[0], step, 0)
+
+
+def forward(emit_seq, init_loc, lengths_loc, trans_loc):
+    steps, seqs, block = emit_seq.shape
+    full = trans_loc.shape[0]
+    col = jnp.broadcast_to(lengths_loc[:, None], (seqs, block))[:, :1]
+    pack = jnp.broadcast_to(lengths_loc.reshape(4, 8).T[:, :, None], (8, 4, 32)).reshape(8, 128)
+    vmem = pl.BlockSpec(memory_space=pltpu.VMEM)
+    hist, scales, log_sum, last = pl.pallas_call(
+        forward_kernel,
+        out_shape=[
+            jax.ShapeDtypeStruct((steps, seqs, block), jnp.bfloat16),
+            jax.ShapeDtypeStruct((steps, 8, 128), jnp.float32),
+            jax.ShapeDtypeStruct((8, 128), jnp.float32),
+            jax.ShapeDtypeStruct((seqs, block), jnp.float32),
+        ],
+        in_specs=[vmem] * 4 + [pl.BlockSpec(memory_space=pltpu.HBM)],
+        out_specs=[vmem] * 4,
+        scratch_shapes=[
+            pltpu.VMEM((full, block), jnp.bfloat16),
+            pltpu.VMEM((2, 4, seqs, block), jnp.bfloat16),
+            pltpu.VMEM((seqs, block), jnp.float32),
+            pltpu.VMEM((4, 8, 128), jnp.float32),
+            pltpu.SemaphoreType.DMA((LOADS,)),
+            pltpu.SemaphoreType.DMA((2, 3, CHUNKS)),
+            pltpu.SemaphoreType.DMA((2, 3, CHUNKS)),
+            pltpu.SemaphoreType.DMA((3,)),
+            pltpu.SemaphoreType.DMA((3,)),
+        ],
+        compiler_params=pltpu.CompilerParams(collective_id=0, has_side_effects=True, vmem_limit_bytes=60 * 1024 * 1024),
+        name="forward",
+    )(emit_seq, init_loc[None, :], col, pack, trans_loc)
+    unpack = lambda x: jnp.swapaxes(x[..., ::32], -1, -2).reshape(x.shape[:-2] + (seqs,))
+    return hist, unpack(scales), unpack(log_sum), last
 
 
 def solution(mesh):
@@ -13,25 +186,11 @@
         seq_count, step_count = tokens_loc.shape
         block_size = trans_loc.shape[1]
         group_idx = lax.axis_index('states')
-        emit_seq = jnp.transpose(jnp.take(emit_loc, tokens_loc.T, axis=1), (1, 2, 0))
-        first_mass = init_loc[None, :] * emit_seq[0].astype(jnp.float32)
-        first_norm = lax.psum(jnp.sum(first_mass, axis=1), 'states')
-        alpha_first = first_mass / first_norm[:, None]
+        emit_seq = jnp.transpose(emit_loc.at[:, tokens_loc.T].get(mode="promise_in_bounds"), (1, 2, 0))
         live_steps = jnp.arange(1, step_count)[:, None] < lengths_loc[None, :]
 
-        def forward_step(alpha_cur, inputs):
-            live_mask, emit_now = inputs
-            alpha_bf = alpha_cur.astype(jnp.bfloat16)
-            alpha_full = lax.all_gather(alpha_bf, 'states', axis=1, tiled=True)
-            pred_mass = jnp.dot(alpha_full, trans_loc, preferred_element_type=jnp.float32)
-            new_mass = pred_mass * emit_now.astype(jnp.float32)
-            norm_sum = lax.psum(jnp.sum(new_mass, axis=1), 'states')
-            step_scale = jnp.where(live_mask, norm_sum, 1.0)
-            alpha_next = jnp.where(live_mask[:, None], new_mass / norm_sum[:, None], alpha_cur)
-            return alpha_next, (alpha_bf, step_scale)
-
-        alpha_last, (alpha_prev, scales) = lax.scan(forward_step, alpha_first, (live_steps, emit_seq[1:]))
-        loglik = jnp.log(first_norm) + jnp.sum(jnp.log(scales), axis=0)
+        hist, all_scales, loglik, alpha_last = forward(emit_seq, init_loc, lengths_loc, trans_loc)
+        alpha_prev, scales = hist[:-1], all_scales[1:]
 
         def backward_step(beta_cur, inputs):
             live_mask, emit_now, step_scale = inputs

time: 4430 us -> 3040 us (0.69)
  blocking collectives: 965 us -> 0 us
  matrix products: 1940 us -> 1050 us
  Pallas kernels: 0 us -> 623 us
  other arithmetic: 312 us -> 169 us
    dot_general x63 -> x0, matrix products: 864 us -> none  [forward_step(): jnp.dot(alpha_full, trans_loc, preferred_element_type=jnp.float32)]
    pallas_call x0 -> x1, Pallas kernels: none -> 623 us  [forward(): pl.pallas_call(forward_kernel, out_shape=[jax.ShapeDtypeStruct((steps, se...]
    all_gather x63 -> x0, blocking collectives: 600 us -> none  [forward_step(): alpha_full = lax.all_gather(alpha_bf, 'states', axis=1, tiled=True)]
    psum x64 -> x0, blocking collectives: 366 us -> none  [the longest x63 357 us: forward_step(): norm_sum = lax.psum(jnp.sum(new_mass, axis=1), 'states')]
  transfers between devices with their start and end apart: 62 -> 62, of which waited for: 62 -> 62; matrix products, arithmetic and copies ran while one was open for 2% -> 3% of each run, Pallas kernels for 0% -> 0%
where the time goes in v1:
time: 3040 us; the launch traced here: 3030 us
  waiting for transfers between devices  1090 us (36%)
  matrix products  1050 us (35%)
  Pallas kernels  623 us (20%)
  other arithmetic  169 us (6%)
  local copies, waits for them, and re-layouts  69.2 us (2%)
    reduce_scatter x62, waiting for transfers between devices, backward_step(): lax.psum_scatter(partial_sum, 'states', scatter_dimension=1, tiled=True)  1090 us
    dot_general x62, matrix products, backward_step(): lax.dot_general(weight, trans_loc, (((1,), (1,)), ((), ())), preferred_el...  1010 us
    pallas_call x1, Pallas kernels, forward(): pl.pallas_call(forward_kernel, out_shape=[jax.ShapeDtypeStruct((steps, se...  623 us
    dynamic_update_slice x62, other arithmetic, local_run(): lax.scan(backward_step, jnp.ones((seq_count, block_size), jnp.float32), (...  103 us
    add x62, other arithmetic, backward_step(): return (beta_prev + jnp.where(live_mask, 0.0, 1.0)[:, None], weight)  64.2 us
  transfers between devices with their start and end apart: 62, of which 62 were waited for; matrix products, arithmetic and copies ran while one was open for 3% of the time, Pallas kernels for 0%

profile of v1, /device:TPU:0, one launch (start us, length us, event | category | flops | bytes accessed | tf_op | source)
XLA Modules:
  0.0 3028.2 jit_solution(18237839387474967631)
XLA Ops:
  12.3 48.0 %gather_fusion = bf16[2048,2048]{1,0:T(8,128)(2,1)} fusion(bf16[2048,10000]{0,1:T(8,128)(2,1)} %param.8, s32[2048]{0:T(1024)S(1)} %broadcast_clamp_fusion), kind=kCustom, calls=%fused_computation | custom fusion | bytes 16785408 | tf_op jit(solution)/shard_map/gather | solution.py:189
  68.5 623.3 %forward.1 = (bf16[64,32,2048]{2,1,0:T(8,128)(2,1)}, f32[64,8,128]{2,1,0:T(8,128)}, f32[8,128]{1,0:T(8,128)}, f32[32,2048]{1,0:T(8,128)}) custom-call(bf16[64,32,2048]{2,1,0:T(8,128)(2,1)} %bitcast.45, f32[1,2048]{1,0:T(1,128)} %bitcast.52, s32[32,1]{1,0:T(8,128)} %copy.16.len_col, s32[8,128]{1,0:T(8,128)} %reshape.47.len_pack, bf16[8192,2048]{1,0:T(8,128)(2,1)} %a_hbm.1), custom_call_target="tpu_custom_call" | custom-call | tf_op jit(solution)/shard_map/forward/pallas_call | solution.py:152
  700.0 2279.4 %while.17 = (s32[]{:T(128)}, f32[32,2048]{1,0:T(8,128)S(1)}, bf16[62,32,2048]{2,1,0:T(8,128)(2,1)}, pred[62,32]{1,0:T(8,128)(4,1)S(1)}, bf16[62,32,2048]{2,1,0:T...) while((s32[]{:T(128)}, f32[32,2048]{1,0:T(8,128)S(1)}, ...), condition=%wide.region_2.3_spmd.clone, body=%wide.region_0.2_spmd.clone.sunk | while | flops 1074593792 | bytes 39978032 | solution.py:202
  718.0 18.2 reduce-scatter.2.cloned.1.call-done
  792.0 17.6 reduce-scatter.2.cloned.1.call-done
  828.8 17.6 reduce-scatter.2.cloned.1.call-done
  902.3 17.6 reduce-scatter.2.cloned.1.call-done
  939.0 17.6 reduce-scatter.2.cloned.1.call-done
  1012.6 17.6 reduce-scatter.2.cloned.1.call-done
  1122.8 17.6 reduce-scatter.2.cloned.1.call-done
  1159.6 17.6 reduce-scatter.2.cloned.1.call-done
  1196.4 17.6 reduce-scatter.2.cloned.1.call-done
  1233.1 17.6 reduce-scatter.2.cloned.1.call-done
  1306.6 17.6 reduce-scatter.2.cloned.1.call-done
  1380.1 17.6 reduce-scatter.2.cloned.1.call-done
  1416.9 17.6 reduce-scatter.2.cloned.1.call-done
  1490.4 17.6 reduce-scatter.2.cloned.1.call-done
  1637.4 17.6 reduce-scatter.2.cloned.1.call-done
  1711.0 17.6 reduce-scatter.2.cloned.1.call-done
  1747.7 17.6 reduce-scatter.2.cloned.1.call-done
  1784.5 17.6 reduce-scatter.2.cloned.1.call-done
  1821.2 17.6 reduce-scatter.2.cloned.1.call-done
  1894.7 17.6 reduce-scatter.2.cloned.1.call-done
  1931.5 17.6 reduce-scatter.2.cloned.1.call-done
  1968.3 17.6 reduce-scatter.2.cloned.1.call-done
  2005.0 17.6 reduce-scatter.2.cloned.1.call-done
  2041.8 17.6 reduce-scatter.2.cloned.1.call-done
  2078.5 17.6 reduce-scatter.2.cloned.1.call-done
  2115.3 17.6 reduce-scatter.2.cloned.1.call-done
  2152.1 17.6 reduce-scatter.2.cloned.1.call-done
  2188.8 17.6 reduce-scatter.2.cloned.1.call-done
  2262.3 17.6 reduce-scatter.2.cloned.1.call-done
  2299.1 17.6 reduce-scatter.2.cloned.1.call-done
  2335.8 17.6 reduce-scatter.2.cloned.1.call-done
  2372.6 17.6 reduce-scatter.2.cloned.1.call-done
  2409.4 17.6 reduce-scatter.2.cloned.1.call-done
  2482.9 17.6 reduce-scatter.2.cloned.1.call-done
  2519.6 17.6 reduce-scatter.2.cloned.1.call-done
  2556.4 17.6 reduce-scatter.2.cloned.1.call-done
  2629.9 17.6 reduce-scatter.2.cloned.1.call-done
  2666.7 17.6 reduce-scatter.2.cloned.1.call-done
  2740.2 17.6 reduce-scatter.2.cloned.1.call-done
  2776.9 17.6 reduce-scatter.2.cloned.1.call-done
  2813.7 17.6 reduce-scatter.2.cloned.1.call-done
  2850.5 17.6 reduce-scatter.2.cloned.1.call-done
  2887.2 17.6 reduce-scatter.2.cloned.1.call-done
  2960.7 17.6 reduce-scatter.2.cloned.1.call-done
  2988.9 32.0 %fusion.6 = f32[2048,2048]{1,0:T(8,128)} fusion(f32[2048,2048]{1,0:T(8,128)} %fusion.10, bf16[64,32,2048]{2,1,0:T(8,128)(2,1)} %get-tuple-element.151, bf16[62,32,2048]{2,1,0:T(8,128)(2,1)} %get-tuple-element.153, bf16[8192,2048]{1,0:T(8,128)(2,1)} %get-tuple-element.286, s32[]{:T(128)S(6)} %select_n.34), kind=kOutput, calls=%fused_computation.13 | convolution fusion | flops 16655581184 | bytes 58458116 | tf_op jit(solution)/shard_map/tbi,tbj->ij/dot_general | solution.py:204
  (484 shorter events, 1530.8 us)
Async XLA Ops:
  700.0 36.2 %reduce-scatter.2.cloned.1.call-start = ((), (), s32[]{:S(2)}) async-start(), calls=%async_computation.1 | async-start | bytes 1310720 | tf_op jit(solution)/shard_map/while/body/eval_jaxpr/reduce_scatter | solution.py:199
  737.2 35.7 %reduce-scatter.2.cloned.1.call-start = ((), (), s32[]{:S(2)}) async-start(), calls=%async_computation.1 | async-start | bytes 1310720 | tf_op jit(solution)/shard_map/while/body/eval_jaxpr/reduce_scatter | solution.py:199
  810.7 35.7 %reduce-scatter.2.cloned.1.call-start = ((), (), s32[]{:S(2)}) async-start(), calls=%async_computation.1 | async-start | bytes 1310720 | tf_op jit(solution)/shard_map/while/body/eval_jaxpr/reduce_scatter | solution.py:199
  847.5 35.7 %reduce-scatter.2.cloned.1.call-start = ((), (), s32[]{:S(2)}) async-start(), calls=%async_computation.1 | async-start | bytes 1310720 | tf_op jit(solution)/shard_map/while/body/eval_jaxpr/reduce_scatter | solution.py:199
  884.2 35.7 %reduce-scatter.2.cloned.1.call-start = ((), (), s32[]{:S(2)}) async-start(), calls=%async_computation.1 | async-start | bytes 1310720 | tf_op jit(solution)/shard_map/while/body/eval_jaxpr/reduce_scatter | solution.py:199
  921.0 35.7 %reduce-scatter.2.cloned.1.call-start = ((), (), s32[]{:S(2)}) async-start(), calls=%async_computation.1 | async-start | bytes 1310720 | tf_op jit(solution)/shard_map/while/body/eval_jaxpr/reduce_scatter | solution.py:199
  957.7 35.7 %reduce-scatter.2.cloned.1.call-start = ((), (), s32[]{:S(2)}) async-start(), calls=%async_computation.1 | async-start | bytes 1310720 | tf_op jit(solution)/shard_map/while/body/eval_jaxpr/reduce_scatter | solution.py:199
  994.5 35.7 %reduce-scatter.2.cloned.1.call-start = ((), (), s32[]{:S(2)}) async-start(), calls=%async_computation.1 | async-start | bytes 1310720 | tf_op jit(solution)/shard_map/while/body/eval_jaxpr/reduce_scatter | solution.py:199
  1031.2 35.7 %reduce-scatter.2.cloned.1.call-start = ((), (), s32[]{:S(2)}) async-start(), calls=%async_computation.1 | async-start | bytes 1310720 | tf_op jit(solution)/shard_map/while/body/eval_jaxpr/reduce_scatter | solution.py:199
  1068.0 35.7 %reduce-scatter.2.cloned.1.call-start = ((), (), s32[]{:S(2)}) async-start(), calls=%async_computation.1 | async-start | bytes 1310720 | tf_op jit(solution)/shard_map/while/body/eval_jaxpr/reduce_scatter | solution.py:199
  1104.8 35.7 %reduce-scatter.2.cloned.1.call-start = ((), (), s32[]{:S(2)}) async-start(), calls=%async_computation.1 | async-start | bytes 1310720 | tf_op jit(solution)/shard_map/while/body/eval_jaxpr/reduce_scatter | solution.py:199
  1141.5 35.7 %reduce-scatter.2.cloned.1.call-start = ((), (), s32[]{:S(2)}) async-start(), calls=%async_computation.1 | async-start | bytes 1310720 | tf_op jit(solution)/shard_map/while/body/eval_jaxpr/reduce_scatter | solution.py:199
  1178.3 35.7 %reduce-scatter.2.cloned.1.call-start = ((), (), s32[]{:S(2)}) async-start(), calls=%async_computation.1 | async-start | bytes 1310720 | tf_op jit(solution)/shard_map/while/body/eval_jaxpr/reduce_scatter | solution.py:199
  1215.0 35.7 %reduce-scatter.2.cloned.1.call-start = ((), (), s32[]{:S(2)}) async-start(), calls=%async_computation.1 | async-start | bytes 1310720 | tf_op jit(solution)/shard_map/while/body/eval_jaxpr/reduce_scatter | solution.py:199
  1251.8 35.7 %reduce-scatter.2.cloned.1.call-start = ((), (), s32[]{:S(2)}) async-start(), calls=%async_computation.1 | async-start | bytes 1310720 | tf_op jit(solution)/shard_map/while/body/eval_jaxpr/reduce_scatter | solution.py:199
  1288.6 35.7 %reduce-scatter.2.cloned.1.call-start = ((), (), s32[]{:S(2)}) async-start(), calls=%async_computation.1 | async-start | bytes 1310720 | tf_op jit(solution)/shard_map/while/body/eval_jaxpr/reduce_scatter | solution.py:199
  1325.3 35.7 %reduce-scatter.2.cloned.1.call-start = ((), (), s32[]{:S(2)}) async-start(), calls=%async_computation.1 | async-start | bytes 1310720 | tf_op jit(solution)/shard_map/while/body/eval_jaxpr/reduce_scatter | solution.py:199
  1362.1 35.7 %reduce-scatter.2.cloned.1.call-start = ((), (), s32[]{:S(2)}) async-start(), calls=%async_computation.1 | async-start | bytes 1310720 | tf_op jit(solution)/shard_map/while/body/eval_jaxpr/reduce_scatter | solution.py:199
  1398.8 35.7 %reduce-scatter.2.cloned.1.call-start = ((), (), s32[]{:S(2)}) async-start(), calls=%async_computation.1 | async-start | bytes 1310720 | tf_op jit(solution)/shard_map/while/body/eval_jaxpr/reduce_scatter | solution.py:199
  1435.6 35.7 %reduce-scatter.2.cloned.1.call-start = ((), (), s32[]{:S(2)}) async-start(), calls=%async_computation.1 | async-start | bytes 1310720 | tf_op jit(solution)/shard_map/while/body/eval_jaxpr/reduce_scatter | solution.py:199
  1472.3 35.7 %reduce-scatter.2.cloned.1.call-start = ((), (), s32[]{:S(2)}) async-start(), calls=%async_computation.1 | async-start | bytes 1310720 | tf_op jit(solution)/shard_map/while/body/eval_jaxpr/reduce_scatter | solution.py:199
  1509.1 35.7 %reduce-scatter.2.cloned.1.call-start = ((), (), s32[]{:S(2)}) async-start(), calls=%async_computation.1 | async-start | bytes 1310720 | tf_op jit(solution)/shard_map/while/body/eval_jaxpr/reduce_scatter | solution.py:199
  1545.9 35.7 %reduce-scatter.2.cloned.1.call-start = ((), (), s32[]{:S(2)}) async-start(), calls=%async_computation.1 | async-start | bytes 1310720 | tf_op jit(solution)/shard_map/while/body/eval_jaxpr/reduce_scatter | solution.py:199
  1582.6 35.7 %reduce-scatter.2.cloned.1.call-start = ((), (), s32[]{:S(2)}) async-start(), calls=%async_computation.1 | async-start | bytes 1310720 | tf_op jit(solution)/shard_map/while/body/eval_jaxpr/reduce_scatter | solution.py:199
  1619.4 35.7 %reduce-scatter.2.cloned.1.call-start = ((), (), s32[]{:S(2)}) async-start(), calls=%async_computation.1 | async-start | bytes 1310720 | tf_op jit(solution)/shard_map/while/body/eval_jaxpr/reduce_scatter | solution.py:199
  1656.1 35.7 %reduce-scatter.2.cloned.1.call-start = ((), (), s32[]{:S(2)}) async-start(), calls=%async_computation.1 | async-start | bytes 1310720 | tf_op jit(solution)/shard_map/while/body/eval_jaxpr/reduce_scatter | solution.py:199
  1692.9 35.7 %reduce-scatter.2.cloned.1.call-start = ((), (), s32[]{:S(2)}) async-start(), calls=%async_computation.1 | async-start | bytes 1310720 | tf_op jit(solution)/shard_map/while/body/eval_jaxpr/reduce_scatter | solution.py:199
  1729.6 35.7 %reduce-scatter.2.cloned.1.call-start = ((), (), s32[]{:S(2)}) async-start(), calls=%async_computation.1 | async-start | bytes 1310720 | tf_op jit(solution)/shard_map/while/body/eval_jaxpr/reduce_scatter | solution.py:199
  1766.4 35.7 %reduce-scatter.2.cloned.1.call-start = ((), (), s32[]{:S(2)}) async-start(), calls=%async_computation.1 | async-start | bytes 1310720 | tf_op jit(solution)/shard_map/while/body/eval_jaxpr/reduce_scatter | solution.py:199
  1803.2 35.7 %reduce-scatter.2.cloned.1.call-start = ((), (), s32[]{:S(2)}) async-start(), calls=%async_computation.1 | async-start | bytes 1310720 | tf_op jit(solution)/shard_map/while/body/eval_jaxpr/reduce_scatter | solution.py:199
  1839.9 35.7 %reduce-scatter.2.cloned.1.call-start = ((), (), s32[]{:S(2)}) async-start(), calls=%async_computation.1 | async-start | bytes 1310720 | tf_op jit(solution)/shard_map/while/body/eval_jaxpr/reduce_scatter | solution.py:199
  1876.7 35.7 %reduce-scatter.2.cloned.1.call-start = ((), (), s32[]{:S(2)}) async-start(), calls=%async_computation.1 | async-start | bytes 1310720 | tf_op jit(solution)/shard_map/while/body/eval_jaxpr/reduce_scatter | solution.py:199
  1913.4 35.7 %reduce-scatter.2.cloned.1.call-start = ((), (), s32[]{:S(2)}) async-start(), calls=%async_computation.1 | async-start | bytes 1310720 | tf_op jit(solution)/shard_map/while/body/eval_jaxpr/reduce_scatter | solution.py:199
  1950.2 35.7 %reduce-scatter.2.cloned.1.call-start = ((), (), s32[]{:S(2)}) async-start(), calls=%async_computation.1 | async-start | bytes 1310720 | tf_op jit(solution)/shard_map/while/body/eval_jaxpr/reduce_scatter | solution.py:199
  2023.7 35.7 %reduce-scatter.2.cloned.1.call-start = ((), (), s32[]{:S(2)}) async-start(), calls=%async_computation.1 | async-start | bytes 1310720 | tf_op jit(solution)/shard_map/while/body/eval_jaxpr/reduce_scatter | solution.py:199
  2060.5 35.7 %reduce-scatter.2.cloned.1.call-start = ((), (), s32[]{:S(2)}) async-start(), calls=%async_computation.1 | async-start | bytes 1310720 | tf_op jit(solution)/shard_map/while/body/eval_jaxpr/reduce_scatter | solution.py:199
  2170.7 35.7 %reduce-scatter.2.cloned.1.call-start = ((), (), s32[]{:S(2)}) async-start(), calls=%async_computation.1 | async-start | bytes 1310720 | tf_op jit(solution)/shard_map/while/body/eval_jaxpr/reduce_scatter | solution.py:199
  2207.5 35.7 %reduce-scatter.2.cloned.1.call-start = ((), (), s32[]{:S(2)}) async-start(), calls=%async_computation.1 | async-start | bytes 1310720 | tf_op jit(solution)/shard_map/while/body/eval_jaxpr/reduce_scatter | solution.py:199
  2317.8 35.7 %reduce-scatter.2.cloned.1.call-start = ((), (), s32[]{:S(2)}) async-start(), calls=%async_computation.1 | async-start | bytes 1310720 | tf_op jit(solution)/shard_map/while/body/eval_jaxpr/reduce_scatter | solution.py:199
  2354.5 35.7 %reduce-scatter.2.cloned.1.call-start = ((), (), s32[]{:S(2)}) async-start(), calls=%async_computation.1 | async-start | bytes 1310720 | tf_op jit(solution)/shard_map/while/body/eval_jaxpr/reduce_scatter | solution.py:199
  2428.0 35.7 %reduce-scatter.2.cloned.1.call-start = ((), (), s32[]{:S(2)}) async-start(), calls=%async_computation.1 | async-start | bytes 1310720 | tf_op jit(solution)/shard_map/while/body/eval_jaxpr/reduce_scatter | solution.py:199
  2464.8 35.7 %reduce-scatter.2.cloned.1.call-start = ((), (), s32[]{:S(2)}) async-start(), calls=%async_computation.1 | async-start | bytes 1310720 | tf_op jit(solution)/shard_map/while/body/eval_jaxpr/reduce_scatter | solution.py:199
  2575.1 35.7 %reduce-scatter.2.cloned.1.call-start = ((), (), s32[]{:S(2)}) async-start(), calls=%async_computation.1 | async-start | bytes 1310720 | tf_op jit(solution)/shard_map/while/body/eval_jaxpr/reduce_scatter | solution.py:199
  2611.8 35.7 %reduce-scatter.2.cloned.1.call-start = ((), (), s32[]{:S(2)}) async-start(), calls=%async_computation.1 | async-start | bytes 1310720 | tf_op jit(solution)/shard_map/while/body/eval_jaxpr/reduce_scatter | solution.py:199
  2722.1 35.7 %reduce-scatter.2.cloned.1.call-start = ((), (), s32[]{:S(2)}) async-start(), calls=%async_computation.1 | async-start | bytes 1310720 | tf_op jit(solution)/shard_map/while/body/eval_jaxpr/reduce_scatter | solution.py:199
  2758.9 35.7 %reduce-scatter.2.cloned.1.call-start = ((), (), s32[]{:S(2)}) async-start(), calls=%async_computation.1 | async-start | bytes 1310720 | tf_op jit(solution)/shard_map/while/body/eval_jaxpr/reduce_scatter | solution.py:199
  2869.1 35.7 %reduce-scatter.2.cloned.1.call-start = ((), (), s32[]{:S(2)}) async-start(), calls=%async_computation.1 | async-start | bytes 1310720 | tf_op jit(solution)/shard_map/while/body/eval_jaxpr/reduce_scatter | solution.py:199
  2905.9 35.7 %reduce-scatter.2.cloned.1.call-start = ((), (), s32[]{:S(2)}) async-start(), calls=%async_computation.1 | async-start | bytes 1310720 | tf_op jit(solution)/shard_map/while/body/eval_jaxpr/reduce_scatter | solution.py:199
  (16 other events, 2811.3 us)
Sparse Core Ops, SparseCore 0:
  716.4 19.6 reduce-scatter.1
  753.7 19.1 reduce-scatter.1
  790.5 19.1 reduce-scatter.1
  827.2 19.1 reduce-scatter.1
  864.0 19.1 reduce-scatter.1
  900.8 19.1 reduce-scatter.1
  937.5 19.1 reduce-scatter.1
  974.3 19.1 reduce-scatter.1
  1011.0 19.1 reduce-scatter.1
  1047.8 19.1 reduce-scatter.1
  1084.5 19.1 reduce-scatter.1
  1121.3 19.1 reduce-scatter.1
  1158.1 19.1 reduce-scatter.1
  1194.8 19.1 reduce-scatter.1
  1231.6 19.1 reduce-scatter.1
  1268.3 19.1 reduce-scatter.1
  1305.1 19.1 reduce-scatter.1
  1341.8 19.1 reduce-scatter.1
  1378.6 19.1 reduce-scatter.1
  1415.4 19.1 reduce-scatter.1
  1452.1 19.1 reduce-scatter.1
  1488.9 19.1 reduce-scatter.1
  1525.6 19.1 reduce-scatter.1
  1562.4 19.1 reduce-scatter.1
  1599.2 19.1 reduce-scatter.1
  1635.9 19.1 reduce-scatter.1
  1672.7 19.1 reduce-scatter.1
  1709.4 19.1 reduce-scatter.1
  1746.2 19.1 reduce-scatter.1
  1782.9 19.1 reduce-scatter.1
  1819.7 19.1 reduce-scatter.1
  1856.5 19.1 reduce-scatter.1
  1893.2 19.1 reduce-scatter.1
  1930.0 19.1 reduce-scatter.1
  1966.7 19.1 reduce-scatter.1
  2003.5 19.1 reduce-scatter.1
  2040.2 19.1 reduce-scatter.1
  2077.0 19.1 reduce-scatter.1
  2113.8 19.1 reduce-scatter.1
  2150.5 19.1 reduce-scatter.1
  2187.3 19.1 reduce-scatter.1
  2224.0 19.1 reduce-scatter.1
  2260.8 19.1 reduce-scatter.1
  2297.6 19.1 reduce-scatter.1
  2334.3 19.1 reduce-scatter.1
  2371.1 19.1 reduce-scatter.1
  2407.8 19.1 reduce-scatter.1
  2444.6 19.1 reduce-scatter.1
  (14 shorter events, 267.0 us)

commit v2 on v1

v2 whole, which is shorter than its diff:
```python
import functools

import jax
import jax.numpy as jnp
from jax import lax
from jax.experimental import pallas as pl
from jax.experimental.pallas import tpu as pltpu
from jax.sharding import PartitionSpec as P

MESH = pl.DeviceIdType.MESH
CHUNKS = 4
LOADS = 8
TILE = 256


def peers(me):
    return me + 1 - 2 * (me % 2), 3 - me, 3 - (me + 1 - 2 * (me % 2))


def entry_barrier(others):
    barrier = pltpu.get_barrier_semaphore()
    for other in others:
        pl.semaphore_signal(barrier, inc=1, device_id=other, device_id_type=MESH)
    pl.semaphore_wait(barrier, len(others))


def exchange_matmul(me, slot, xbuf, mat, acc, send_sem, recv_sem, meanwhile):
    partner, cross, far = peers(me)
    block = xbuf.shape[3]
    width = block // CHUNKS

    def part(owner, c):
        return xbuf.at[slot, owner, :, pl.ds(c * width, width)]

    def copy(owner, c, kind, device):
        ref = part(owner, c)
        return pltpu.make_async_remote_copy(
            src_ref=ref, dst_ref=ref, send_sem=send_sem.at[slot, kind, c], recv_sem=recv_sem.at[slot, kind, c],
            device_id={"states": device}, device_id_type=MESH)

    sends = []
    for c in range(CHUNKS):
        out = copy(me, c, 1, cross)
        out.start()
        sends.append(out)
        out = copy(me, c, 0, partner)
        out.start()
        sends.append(out)
    meanwhile()

    def dot(owner, lo, size):
        rows = pl.ds(pl.multiple_of(owner * block + lo, width), size)
        return jnp.dot(xbuf[slot, owner, :, pl.ds(lo, size)], mat[rows, :], preferred_element_type=jnp.float32)

    acc[...] = dot(me, 0, block)
    for c in range(CHUNKS):
        copy(partner, c, 0, partner).wait_recv()
    acc[...] += dot(partner, 0, block)

    def relay(c):
        copy(cross, c, 1, cross).wait_recv()
        out = copy(cross, c, 2, partner)
        out.start()
        sends.append(out)

    for c in range(CHUNKS):
        relay(c)
        acc[...] += dot(cross, c * width, width)
        if c:
            copy(far, c - 1, 2, partner).wait_recv()
            acc[...] += dot(far, (c - 1) * width, width)
    copy(far, CHUNKS - 1, 2, partner).wait_recv()
    acc[...] += dot(far, (CHUNKS - 1) * width, width)
    return sends


def packed(col):
    group = lax.broadcasted_iota(jnp.int32, (8, 128), 1) // 32
    out = jnp.broadcast_to(col[24:32], (8, 128))
    for k in range(3):
        out = jnp.where(group == k, jnp.broadcast_to(col[8 * k:8 * k + 8], (8, 128)), out)
    return out


def unpacked(tile):
    return jnp.concatenate([tile[:, 32 * k:32 * k + 1] for k in range(4)], axis=0)


def forward_kernel(emit_ref, init_ref, len_col, len_pack, a_hbm, hist_ref, scale_ref, log_ref, post_ref, rows_hbm,
                   mat, xbuf, acc, cbuf, load_sem, send_sem, recv_sem, csend_sem, crecv_sem,
                   over_send, over_recv, turn_send, turn_recv, near_send, near_recv):
    me, seq = lax.axis_index("states"), lax.axis_index("seqs")
    partner, cross, far = peers(me)
    steps, _, block = emit_ref.shape
    rows = mat.shape[0] // LOADS
    loads = [pltpu.make_async_copy(a_hbm.at[pl.ds(k * rows, rows)], mat.at[pl.ds(k * rows, rows)], load_sem.at[k]) for k in range(LOADS)]
    for load in loads:
        load.start()
    entry_barrier([{"states": partner}, {"states": cross}, {"states": far}, {"seqs": 1 - seq}])

    half = block // 2
    piece = half // steps

    def over(b, kind, owner, other):
        lo = seq * half + b * piece
        return pltpu.make_async_remote_copy(
            src_ref=a_hbm.at[pl.ds(other * block + lo, piece)], dst_ref=rows_hbm.at[owner, pl.ds(lo, piece)],
            send_sem=over_send.at[b % 3, kind], recv_sem=over_recv.at[b % 3, kind], device_id={"states": other}, device_id_type=MESH)

    def turn(b, kind, owner):
        ref = rows_hbm.at[owner, pl.ds(seq * half + b * piece, piece)]
        return pltpu.make_async_remote_copy(
            src_ref=ref, dst_ref=ref, send_sem=turn_send.at[b % 2, kind], recv_sem=turn_recv.at[kind],
            device_id={"seqs": 1 - seq}, device_id_type=MESH)

    def near(b):
        return pltpu.make_async_remote_copy(
            src_ref=a_hbm.at[pl.ds(partner * block + b * 2 * piece, 2 * piece)], dst_ref=rows_hbm.at[me, pl.ds(b * 2 * piece, 2 * piece)],
            send_sem=near_send.at[b % 2], recv_sem=near_recv, device_id={"states": partner}, device_id_type=MESH)

    others = ((0, cross), (1, far))

    def rows_start(b):
        for kind, other in others:
            over(b, kind, me, other).start()
        near(b).start()

    def rows_turn(b):
        near(b).wait_send()
        for kind, other in others:
            over(b, kind, me, other).wait_send()
            over(b, kind, other, other).wait_recv()
            turn(b, kind, other).start()

    def rows_end(b):
        for kind, other in others:
            turn(b, kind, other).wait_send()

    def norm_total(mass):
        cbuf[me] = packed(jnp.sum(mass, axis=1, keepdims=True))

        def copy(owner, kind, device):
            return pltpu.make_async_remote_copy(
                src_ref=cbuf.at[owner], dst_ref=cbuf.at[owner], send_sem=csend_sem.at[kind], recv_sem=crecv_sem.at[kind],
                device_id={"states": device}, device_id_type=MESH)

        return [(copy(me, kind, other), copy(other, kind, other)) for kind, other in enumerate((far, cross, partner))]

    def norm_end(pairs):
        for _, arrive in pairs:
            arrive.wait_recv()
        for leave, _ in pairs:
            leave.wait_send()
        return cbuf[0] + cbuf[1] + cbuf[2] + cbuf[3]

    mass = init_ref[...] * emit_ref[0].astype(jnp.float32)
    pairs = norm_total(mass)
    for leave, _ in pairs:
        leave.start()
    rows_start(0)
    total = norm_end(pairs)
    scale_ref[0] = total
    log_ref[...] = jnp.log(total)
    alpha = mass * unpacked(1.0 / total)
    post_ref[...] = alpha
    xbuf[0, me] = alpha.astype(jnp.bfloat16)
    hist_ref[1] = alpha.astype(jnp.bfloat16)
    for load in loads:
        load.wait()

    def step(t, carry):
        slot = (t - 1) % 2
        sends = exchange_matmul(me, slot, xbuf, mat, acc, send_sem, recv_sem, lambda: rows_start(t))
        mass = acc[...] * emit_ref[t].astype(jnp.float32)
        acc[...] = mass
        pairs = norm_total(mass)
        for leave, _ in pairs:
            leave.start()
        for send in sends:
            send.wait_send()
        rows_turn(t - 1)

        @pl.when(t > 1)
        def _():
            rows_end(t - 2)

        total = norm_end(pairs)
        live = t < len_pack[...]
        scale = jnp.where(live, total, 1.0)
        scale_ref[t] = scale
        log_ref[...] += jnp.log(scale)
        alpha = jnp.where(t < len_col[...], acc[...] * unpacked(1.0 / total), post_ref[...])
        post_ref[...] = alpha
        xbuf[t % 2, me] = alpha.astype(jnp.bfloat16)
        hist_ref[(t + 1) % steps] = alpha.astype(jnp.bfloat16)
        return carry

    lax.fori_loop(1, steps, step, 0)
    rows_turn(steps - 1)
    rows_end(steps - 2)
    rows_end(steps - 1)

    def landed(ref, sem):
        pltpu.make_async_copy(ref, ref, sem).wait()

    for kind, other in others:
        landed(rows_hbm.at[other, pl.ds((1 - seq) * half, half)], turn_recv.at[kind])
    landed(rows_hbm.at[partner], near_recv)


def forward(emit_seq, init_loc, col, pack, trans_loc):
    steps, seqs, block = emit_seq.shape
    full = trans_loc.shape[0]
    vmem, hbm = pl.BlockSpec(memory_space=pltpu.VMEM), pl.BlockSpec(memory_space=pltpu.HBM)
    dma = pltpu.SemaphoreType.DMA
    return pl.pallas_call(
        forward_kernel,
        out_shape=[
            jax.ShapeDtypeStruct((steps, seqs, block), jnp.bfloat16),
            jax.ShapeDtypeStruct((steps, 8, 128), jnp.float32),
            jax.ShapeDtypeStruct((8, 128), jnp.float32),
            jax.ShapeDtypeStruct((seqs, block), jnp.float32),
            jax.ShapeDtypeStruct((full // block, block, block), jnp.bfloat16),
        ],
        in_specs=[vmem] * 4 + [hbm],
        out_specs=[vmem] * 4 + [hbm],
        scratch_shapes=[
            pltpu.VMEM((full, block), jnp.bfloat16),
            pltpu.VMEM((2, 4, seqs, block), jnp.bfloat16),
            pltpu.VMEM((seqs, block), jnp.float32),
            pltpu.VMEM((4, 8, 128), jnp.float32),
            dma((LOADS,)), dma((2, 3, CHUNKS)), dma((2, 3, CHUNKS)), dma((3,)), dma((3,)),
            dma((3, 2)), dma((3, 2)), dma((2, 2)), dma((2,)), dma((2,)), dma,
        ],
        compiler_params=pltpu.CompilerParams(collective_id=0, has_side_effects=True, vmem_limit_bytes=60 * 1024 * 1024),
        name="forward",
    )(emit_seq, init_loc[None, :], col, pack, trans_loc)


def backward_kernel(emit_ref, scale_ref, len_col, a_hbm, rows_hbm, hist_ref, mat, xbuf, acc, coef, load_sem, send_sem, recv_sem):
    me = lax.axis_index("states")
    partner, cross, far = peers(me)
    steps, _, block = emit_ref.shape
    owners = (me, partner, cross, far)
    loads = []
    for k, owner in enumerate(owners):
        src = a_hbm.at[pl.ds(me * block, block)] if k == 0 else rows_hbm.at[owner]
        loads.append(pltpu.make_async_copy(src, mat.at[pl.ds(owner * block, block)], load_sem.at[k]))
        loads[-1].start()
    entry_barrier([{"states": partner}, {"states": cross}, {"states": far}])

    def weigh(t):
        inv = jnp.where(t < len_col[...], unpacked(1.0 / scale_ref[t]), 0.0)
        coef[...] = emit_ref[t].astype(jnp.float32) * inv

    def emit_weight(t, weight):
        xbuf[t % 2, me] = weight.astype(jnp.bfloat16)
        hist_ref[t] = weight.astype(jnp.bfloat16)

    weigh(steps - 1)
    emit_weight(steps - 1, coef[...])
    hist_ref[0] = jnp.zeros(hist_ref.shape[1:], hist_ref.dtype)

    side = block // TILE
    for owner, load in zip(owners, loads):
        load.wait()

        def flip_row(r, carry):
            def flip(c, inner):
                def tile(p, q):
                    return pl.ds(pl.multiple_of(owner * block + p * TILE, TILE), TILE), pl.ds(pl.multiple_of(q * TILE, TILE), TILE)

                upper, lower = mat[tile(r, c)], mat[tile(c, r)]
                mat[tile(r, c)] = lower.T
                mat[tile(c, r)] = upper.T
                return inner

            return lax.fori_loop(r, side, flip, carry)

        lax.fori_loop(0, side, flip_row, 0)

    def step(k, carry):
        t = steps - 1 - k
        sends = exchange_matmul(me, t % 2, xbuf, mat, acc, send_sem, recv_sem, lambda: weigh(t - 1))
        beta = acc[...] + jnp.where(t < len_col[...], 0.0, 1.0)
        emit_weight(t - 1, coef[...] * beta)
        for send in sends:
            send.wait_send()
        return carry

    lax.fori_loop(0, steps - 2, step, 0)


def backward(emit_seq, scales, col, trans_loc, rows_loc):
    steps, seqs, block = emit_seq.shape
    full = trans_loc.shape[0]
    vmem, hbm = pl.BlockSpec(memory_space=pltpu.VMEM), pl.BlockSpec(memory_space=pltpu.HBM)
    dma = pltpu.SemaphoreType.DMA
    return pl.pallas_call(
        backward_kernel,
        out_shape=jax.ShapeDtypeStruct((steps, seqs, block), jnp.bfloat16),
        in_specs=[vmem] * 3 + [hbm] * 2,
        out_specs=vmem,
        scratch_shapes=[
            pltpu.VMEM((full, block), jnp.bfloat16),
            pltpu.VMEM((2, 4, seqs, block), jnp.bfloat16),
            pltpu.VMEM((seqs, block), jnp.float32),
            pltpu.VMEM((seqs, block), jnp.float32),
            dma((4,)), dma((2, 3, CHUNKS)), dma((2, 3, CHUNKS)),
        ],
        compiler_params=pltpu.CompilerParams(collective_id=1, has_side_effects=True, vmem_limit_bytes=60 * 1024 * 1024),
        name="backward",
    )(emit_seq, scales, col, trans_loc, rows_loc)


def solution(mesh):
    def local_run(trans_loc, emit_loc, init_loc, tokens_loc, lengths_loc):
        seqs, steps = tokens_loc.shape
        block = trans_loc.shape[1]
        emit_seq = jnp.transpose(emit_loc.at[:, tokens_loc.T].get(mode="promise_in_bounds"), (1, 2, 0))
        col = lengths_loc[:, None]
        pack = jnp.broadcast_to(lengths_loc.reshape(4, 8).T[:, :, None], (8, 4, 32)).reshape(8, 128)
        alphas, scales, log_sum, last, rows_loc = forward(emit_seq, init_loc, col, pack, trans_loc)
        weights = backward(emit_seq, scales, col, trans_loc, rows_loc)
        pair_sum = lax.dot_general(alphas.reshape(steps * seqs, block), weights.reshape(steps * seqs, block), (((0,), (0,)), ((), ())), preferred_element_type=jnp.float32)
        diag_block = lax.dynamic_slice_in_dim(trans_loc, lax.axis_index('states') * block, block, axis=0)
        counts = diag_block.astype(jnp.float32) * pair_sum
        return log_sum[:, ::32].T.reshape(seqs), last, counts

    return jax.shard_map(local_run, mesh=mesh, in_specs=(P(None, 'states'), P('states', None), P('states'), P('seqs', None), P('seqs')), out_specs=(P('seqs'), P('seqs', 'states'), P(('seqs', 'states'), None)), check_vma=False)
```

time: 3040 us -> 1160 us (0.38)
  waiting for transfers between devices: 1090 us -> 0 us
  matrix products: 1050 us -> 25.2 us
  Pallas kernels: 623 us -> 1080 us
  other arithmetic: 169 us -> 0.73 us
    reduce_scatter x62 -> x0, waiting for transfers between devices: 1090 us -> none  [backward_step(): lax.psum_scatter(partial_sum, 'states', scatter_dimension=1, tiled=True)]
    dot_general x64 -> x1, matrix products: 1050 us -> 25.2 us  [local_run(): lax.dot_general(alphas.reshape(steps * seqs, block), weights.reshape(step...]
    pallas_call x0 -> x1, Pallas kernels: none -> 446 us  [backward(): pl.pallas_call(backward_kernel, out_shape=jax.ShapeDtypeStruct((steps, se...]
    dynamic_update_slice x62 -> x0, other arithmetic: 103 us -> none  [local_run(): lax.scan(backward_step, jnp.ones((seq_count, block_size), jnp.float32), (...]
    add x63 -> x0, other arithmetic: 64.2 us -> none  [the longest x62 64.2 us: backward_step(): return (beta_prev + jnp.where(live_mask, 0.0, 1.0)[:, None], weight)]
  transfers between devices with their start and end apart: 62 -> 0, of which waited for: 62 -> 0; matrix products, arithmetic and copies ran while one was open for 3% -> 0% of each run, Pallas kernels for 0% -> 0%
where the time goes in v2:
time: 1160 us
  Pallas kernels  1080 us (93%)
  local copies, waits for them, and re-layouts  51.9 us (4%)
  matrix products  25.2 us (2%)
    pallas_call x1, Pallas kernels, forward(): pl.pallas_call(forward_kernel, out_shape=[jax.ShapeDtypeStruct((steps, se...  633 us
    pallas_call x1, Pallas kernels, backward(): pl.pallas_call(backward_kernel, out_shape=jax.ShapeDtypeStruct((steps, se...  446 us
    gather x1, local copies, waits for them, and re-layouts, local_run(): emit_loc.at[:, tokens_loc.T].get(mode='promise_in_bounds')  47.9 us
    dot_general x1, matrix products, local_run(): lax.dot_general(alphas.reshape(steps * seqs, block), weights.reshape(step...  25.2 us

profile of v2, /device:TPU:0, one launch (start us, length us, event | category | flops | bytes accessed | tf_op | source)
XLA Modules:
  0.0 1157.6 jit_solution(3203739700561247693)
XLA Ops:
  0.6 0.7 compare_select_fusion
  1.4 0.1 copy.14
  1.4 0.1 reshape.23
  1.5 0.0 copy-start.1
  1.5 47.9 %gather_fusion = bf16[2048,2048]{1,0:T(8,128)(2,1)} fusion(bf16[2048,10000]{0,1:T(8,128)(2,1)} %param.6, s32[2048]{0:T(1024)S(1)} %broadcast_clamp_fusion), kind=kCustom, calls=%fused_computation | custom fusion | bytes 16785408 | tf_op jit(solution)/shard_map/gather | solution.py:320
  49.5 0.0 copy-done.1
  49.5 0.7 copy.16.len_col
  50.2 0.1 reshape.18
  50.2 0.1 copy.15
  50.3 0.1 broadcast_in_dim.18
  50.4 0.7 reshape.19.len_pack
  51.1 632.8 %forward.1 = (bf16[64,32,2048]{2,1,0:T(8,128)(2,1)}, f32[64,8,128]{2,1,0:T(8,128)}, f32[8,128]{1,0:T(8,128)}, f32[32,2048]{1,0:T(8,128)}, bf16[4,2048,2048]{2,1,0:T(8,128)(2,1)}) custom-call(bf16[64,32,2048]{2,1,0:T(8,128)(2,1)} %bitcast.11, f32[1,2048]{1,0:T(1,128)} %bitcast.15, s32[32,1]{1,0:T(8,128)} %copy.16.len_col, s32[8,128]{1,0:T(8,128)} %reshape.19.len_pack, ...), custom_call_target="tpu_custom_call" | custom-call | tf_op jit(solution)/shard_map/forward/pallas_call | solution.py:216
  683.9 0.8 slice.3
  684.6 0.1 copy.17
  684.7 0.6 reshape.20
  685.3 446.3 %backward.1 = bf16[64,32,2048]{2,1,0:T(8,128)(2,1)} custom-call(bf16[64,32,2048]{2,1,0:T(8,128)(2,1)} %bitcast.12, f32[64,8,128]{2,1,0:T(8,128)} %get-tuple-element.11.scale_ref, s32[32,1]{1,0:T(8,128)} %copy.16.len_col, bf16[8192,2048]{1,0:T(8,128)(2,1)} %a_hbm.3, bf16[4,2048,2048]{2,1,0:T(8,128)(2,1)} %get-tuple-element.12.rows_hbm), custom_call_target="tpu_custom_call" | custom-call | tf_op jit(solution)/shard_map/backward/pallas_call | solution.py:299
  1131.6 0.0 copy-start
  1131.6 25.2 %bitcast_multiply_fusion = f32[2048,2048]{1,0:T(8,128)} fusion(bf16[64,32,2048]{2,1,0:T(8,128)(2,1)} %get-tuple-element.10, bf16[64,32,2048]{2,1,0:T(8,128)(2,1)} %backward.1, bf16[8192,2048]{1,0:T(8,128)(2,1)} %a_hbm.3, s32[]{:T(128)S(6)} %select_n.7), kind=kOutput, calls=%fused_computation.1 | convolution fusion | flops 17188257792 | bytes 41943044 | tf_op jit(solution)/shard_map/dot_general | solution.py:325
  1156.9 0.0 copy-done
  1156.9 0.7 copy.24
  (1 shorter events, 0.0 us)
Async XLA Ops:
  1.5 48.0 %copy-start.1 = (s32[32]{0:T(128)S(1)}, s32[32]{0:T(128)}, u32[]{:S(2)}) copy-start(s32[32]{0:T(128)} %param.9) | copy-start | bytes 388
  1131.6 25.3 %copy-start = (f32[32,2048]{1,0:T(8,128)S(1)}, f32[32,2048]{1,0:T(8,128)}, u32[]{:S(2)}) copy-start(f32[32,2048]{1,0:T(8,128)} %get-tuple-element.17) | copy-start | bytes 786436
